TPU v7x, 32 devices: a 4x4x1 block of a 4x4x8 slice. The times are simulated.
32 devices in a mesh: data: 1 (over z), seq: 32 (over y, x, core).
Axes of the slice: x: 4, y: 4, z: 1, core: 2. Of those that a mesh axis runs over, the one named last changes fastest.
The devices are a block of a 4x4x8 slice.
Arguments:
- x: bfloat16 [2048, 2560], P(('data', 'seq'))
- g1: float32 [2560], replicated
- b1: float32 [2560], replicated
- g2: float32 [2560], replicated
- b2: float32 [2560], replicated
- wqkv: bfloat16 [2560, 7680], replicated
- wo: bfloat16 [32, 80, 2560], replicated
- w1: bfloat16 [2560, 10240], replicated
- w2: bfloat16 [10240, 2560], replicated
Outputs:
- output: bfloat16 [2048, 2560], P(('data', 'seq'))
All inputs are finite; a program needn't handle non-finite values.
Results may differ from a plain program's by a relative error of at most 0.00237603.
Values are sent between devices in bfloat16 or wider.
A program may use at most 768 MiB of HBM per device.

v0:
```python
import jax
import jax.numpy as jnp
from jax import lax
from jax.sharding import PartitionSpec as P

QROWS = 128
EPS = 1e-5
NEG = -1e30
F32 = jnp.float32
BF16 = jnp.bfloat16


def _stats(x):
    xf = x.astype(F32)
    mu = jnp.mean(xf, axis=-1, keepdims=True)
    var = jnp.mean(jnp.square(xf - mu), axis=-1, keepdims=True)
    return mu, lax.rsqrt(var + EPS)


def _norm(x, st, g, b):
    mu, rs = st
    return ((x.astype(F32) - mu) * rs * g + b).astype(BF16)


def _rope_tables(pos, dh):
    half = dh // 2
    inv = 10000.0 ** (-2.0 * jnp.arange(half, dtype=F32) / dh)
    ang = pos.astype(F32)[:, None] * inv[None, :]
    return jnp.cos(ang)[:, None, None, :], jnp.sin(ang)[:, None, None, :]


def _rope_qkv(t, cs):
    cos, sin = cs
    half = t.shape[-1] // 2
    tf = t[:, :2].astype(F32)
    a, b = tf[..., :half], tf[..., half:]
    qk = jnp.concatenate([a * cos - b * sin, b * cos + a * sin], axis=-1).astype(BF16)
    return jnp.concatenate([qk, t[:, 2:]], axis=1).transpose(1, 0, 2, 3)


def _attend(q, k, v, q0, rb):
    nh, n, dh = q.shape
    nk = k.shape[1]
    scale = dh ** -0.5

    def block(qb, p0, kn):
        sc = jnp.einsum("hqe,hke->hqk", qb, k[:, :kn], preferred_element_type=F32) * scale
        rows = p0 + lax.broadcasted_iota(jnp.int32, sc.shape, 1)
        cols = lax.broadcasted_iota(jnp.int32, sc.shape, 2)
        sc = jnp.where(cols <= rows, sc, NEG)
        p = jax.nn.softmax(sc, axis=-1).astype(BF16)
        return jnp.einsum("hqk,hke->qhe", p, v[:, :kn], preferred_element_type=F32).astype(BF16)

    if isinstance(q0, int):
        return jnp.concatenate(
            [block(q[:, i:i + rb], q0 + i, min(nk, q0 + i + rb)) for i in range(0, n, rb)], axis=0)

    def step(i):
        return block(lax.dynamic_slice_in_dim(q, i * rb, rb, axis=1), q0 + i * rb, nk)

    return lax.map(step, jnp.arange(n // rb)).reshape(n, nh, dh)


def solution(mesh):
    nseq = mesh.shape["seq"]

    def local(x, g1, b1, g2, b2, wqkv, wo, w1, w2):
        r, d = x.shape
        nh, dh, _ = wo.shape
        pos = lax.axis_index("seq") * r + jnp.arange(r)
        st = _stats(x)
        a = _norm(x, st, g1, b1)
        qkv = jnp.dot(a, wqkv, preferred_element_type=F32).astype(BF16).reshape(r, 3, nh, dh)
        qkv = _rope_qkv(qkv, _rope_tables(pos, dh))
        qkv = lax.all_to_all(qkv, "seq", 2, 1, tiled=True)
        t = qkv.transpose(0, 2, 1, 3)
        o = _attend(t[0], t[1], t[2], 0, QROWS)
        o = lax.all_to_all(o, "seq", 0, 1, tiled=True)
        attn = jnp.dot(o.reshape(r, nh * dh), wo.reshape(nh * dh, d), preferred_element_type=F32)
        m = _norm(x, st, g2, b2)
        h = jax.nn.gelu(jnp.dot(m, w1, preferred_element_type=F32), approximate=False).astype(BF16)
        mlp = jnp.dot(h, w2, preferred_element_type=F32)
        return (x.astype(F32) + attn + mlp).astype(BF16)

    rows = P(("data", "seq"), None)
    rep = P()
    return jax.shard_map(local, mesh=mesh,
                         in_specs=(rows, rep, rep, rep, rep, rep, rep, rep, rep),
                         out_specs=rows, check_vma=False)
```

profile of v0, /device:TPU:97, one launch (start us, length us, event | category | flops | bytes accessed | tf_op | source)
XLA Modules:
  0.0 136.0 jit_solution(62081761351787506)
XLA Ops:
  0.0 1.1 convert_reduce_fusion
  1.1 1.2 fusion.103
  2.4 16.0 %convolution_convert_fusion = bf16[64,7680]{1,0:T(8,128)(2,1)S(1)} fusion(bf16[2560,7680]{1,0:T(8,128)(2,1)} %param.14, bf16[64,2560]{1,0:T(8,128)(2,1)} %param.9, f32[2560]{0:T(1024)} %param.11, f32[2560]{0:T(1024)} %param.10, f32[64]{0:T(128)S(1)} %add_rsqrt_fusion, f32[64]{0:T(128)S(1)} %broadcast_multiply_fusion), kind=kOutput, calls=%fused_computation | convolution fusion | flops 2518056960 | bytes 40653312 | tf_op jit(solution)/shard_map/dot_general | solution.py:73
  18.4 2.0 %reshape.605 = bf16[64,3,32,80]{3,2,1,0:T(8,128)(2,1)S(1)} reshape(bf16[64,7680]{1,0:T(8,128)(2,1)S(1)} %convolution_convert_fusion) | data formatting | bytes 1966080 | tf_op jit(solution)/shard_map/reshape | solution.py:73
  20.8 0.6 copy_convert_fusion
  21.6 0.8 subtract_convert_fusion
  22.4 1.9 %maximum_bitcast_fusion = bf16[3,64,32,80]{3,1,0,2:T(8,128)(2,1)} fusion(bf16[64,1,32,80]{3,0,1,2:T(8,128)(2,1)S(1)} %copy.29, bf16[64,2,32,40]{3,0,1,2:T(8,128)(2,1)S(1)} %get-tuple-element.6, bf16[64,2,32,40]{3,0,1,2:T(8,128)(2,1)S(1)} %get-tuple-element.5), kind=kLoop, calls=%fused_computation.41 | loop fusion | flops 2949120 | bytes 1966080 | tf_op jit(solution)/shard_map/transpose | solution.py:38
  24.3 9.2 %all-to-all-start = ((bf16[3,64,32,80]{3,1,0,2:T(8,128)(2,1)}), bf16[3,64,32,80]{3,1,0,2:T(8,128)(2,1)S(1)}, u32[]{:S(2)}, u32[]{:S(2)}) async-start(bf16[3,64,32,80]{3,1,0,2:T(8,128)(2,1)} %maximum_bitcast_fusion), calls=%async_computation | async-start | bytes 3145728 | tf_op jit(solution)/shard_map/all_to_all | solution.py:75
  33.7 22.8 %all-to-all-done = bf16[3,64,32,80]{3,1,0,2:T(8,128)(2,1)S(1)} async-done(((bf16[3,64,32,80]{3,1,0,2:T(8,128)(2,1)}), bf16[3,64,32,80]{3,1,0,2:T(8,128)(2,1)S(1)}, u32[]{:S(2)}, u32[]{:S(2)}) %all-to-all-start) | async-done | bytes 983072 | tf_op jit(solution)/shard_map/all_to_all | solution.py:75
  57.0 0.3 fusion.189
  57.6 0.3 fusion.191
  57.9 0.3 fusion.192
  58.2 0.3 fusion.193
  58.5 0.3 fusion.194
  58.8 0.4 fusion.195
  59.2 0.4 fusion.196
  59.6 0.4 fusion.197
  59.9 0.4 fusion.198
  60.3 0.4 fusion.199
  60.7 0.4 fusion.200
  61.1 0.4 fusion.201
  62.9 0.3 fusion.65
  63.4 0.3 fusion.67
  63.9 0.3 fusion.83
  64.5 0.4 fusion.85
  65.1 0.3 fusion.87
  65.6 0.4 fusion.89
  66.2 0.3 fusion.69
  66.8 0.4 fusion.71
  67.5 0.4 fusion.73
  68.1 0.4 fusion.75
  68.8 0.4 fusion.77
  69.2 0.3 fusion.91
  69.5 0.4 fusion.79
  69.9 0.4 fusion.202
  70.4 0.3 fusion.90
  70.7 0.4 fusion.81
  71.1 0.5 broadcast.254
  71.6 0.8 reduce.64
  72.7 1.0 reshape.656
  73.7 12.9 %all_to_all.30 = bf16[32,2,2560]{2,1,0:T(2,128)(2,1)S(1)} all-to-all(bf16[32,2,2560]{2,1,0:T(2,128)(2,1)S(1)} %reshape.656), channel_id=1, replica_groups=mesh['data'=1,'seq'=32] {'seq'}, dimensions={0} | all-to-all | bytes 655360 | tf_op jit(solution)/shard_map/all_to_all | solution.py:78
  86.6 1.1 reshape.657
  87.8 0.6 copy.21
  88.4 0.7 all_to_all.26
  89.1 1.2 copy.22
  90.3 0.8 reshape.654
  91.2 7.1 %convolution_add_fusion = f32[64,2560]{1,0:T(8,128)S(1)} fusion(bf16[64,2560]{1,0:T(8,128)(2,1)S(1)} %reshape.654, bf16[2560,2560]{1,0:T(8,128)(2,1)} %bitcast.367, bf16[64,2560]{1,0:T(8,128)(2,1)S(1)} %copy-done), kind=kOutput, calls=%fused_computation.2 | convolution fusion | flops 839188480 | bytes 14417920 | tf_op jit(solution)/shard_map/dot_general | solution.py:79
  98.3 37.7 %fusion = bf16[64,2560]{1,0:T(8,128)(2,1)} fusion(f32[64,2560]{1,0:T(8,128)S(1)} %convolution_add_fusion, bf16[10240,2560]{1,0:T(8,128)(2,1)} %param.17, bf16[2560,10240]{1,0:T(8,128)(2,1)} %param.16, bf16[64,2560]{1,0:T(8,128)(2,1)S(1)} %copy-done, f32[2560]{0:T(1024)S(1)} %copy-done.1, f32[2560]{0:T(1024)S(1)} %copy-done.2, f32[64]{0:T(128)S(1)} %add_rsqrt_fusion, ...), kind=kOutput, calls=%fused_computation.4 | convolution fusion | flops 6754795520 | bytes 106189312 | tf_op jit(solution)/shard_map/dot_general | solution.py:82
  (51 shorter events, 5.5 us)
Async XLA Ops:
  24.3 32.1 %all-to-all-start = ((bf16[3,64,32,80]{3,1,0,2:T(8,128)(2,1)}), bf16[3,64,32,80]{3,1,0,2:T(8,128)(2,1)S(1)}, u32[]{:S(2)}, u32[]{:S(2)}) async-start(bf16[3,64,32,80]{3,1,0,2:T(8,128)(2,1)} %maximum_bitcast_fusion), calls=%async_computation | async-start | bytes 3145728 | tf_op jit(solution)/shard_map/all_to_all | solution.py:75
  86.6 4.5 %copy-start = (bf16[64,2560]{1,0:T(8,128)(2,1)S(1)}, bf16[64,2560]{1,0:T(8,128)(2,1)}, u32[]{:S(2)}) copy-start(bf16[64,2560]{1,0:T(8,128)(2,1)} %param.9) | copy-start | bytes 983044
  91.2 7.1 %copy-start.1 = (f32[2560]{0:T(1024)S(1)}, f32[2560]{0:T(1024)}, u32[]{:S(2)}) copy-start(f32[2560]{0:T(1024)} %param.13) | copy-start | bytes 30724
  91.2 7.1 %copy-start.2 = (f32[2560]{0:T(1024)S(1)}, f32[2560]{0:T(1024)}, u32[]{:S(2)}) copy-start(f32[2560]{0:T(1024)} %param.12) | copy-start | bytes 30724
where the time goes:
time: 136 us
  matrix products  71.6 us (53%)
  waiting for transfers between devices  22.8 us (17%)
  blocking collectives  12.9 us (9%)
  other arithmetic  10.3 us (8%)
  starting transfers between devices  9.16 us (7%)
  local copies, waits for them, and re-layouts  8.72 us (6%)
    dot_general x1, matrix products, local(): mlp = jnp.dot(h, w2, preferred_element_type=F32)  37.7 us
    all_to_all x1, waiting for transfers between devices, local(): qkv = lax.all_to_all(qkv, 'seq', 2, 1, tiled=True)  22.8 us
    dot_general x1, matrix products, local(): jnp.dot(a, wqkv, preferred_element_type=F32).astype(BF16)  16 us
    all_to_all x1, blocking collectives, local(): o = lax.all_to_all(o, 'seq', 0, 1, tiled=True)  12.9 us
    all_to_all x1, starting transfers between devices, local(): qkv = lax.all_to_all(qkv, 'seq', 2, 1, tiled=True)  9.16 us
    dot_general x1, matrix products, local(): jnp.dot(o.reshape(r, nh * dh), wo.reshape(nh * dh, d), preferred_element_...  7.1 us
    dot_general x16, matrix products, block(): jnp.einsum('hqk,hke->qhe', p, v[:, :kn], preferred_element_type=F32)  5.42 us
    dot_general x16, matrix products, block(): jnp.einsum('hqe,hke->hqk', qb, k[:, :kn], preferred_element_type=F32)  5.38 us
  transfers between devices with their start and end apart: 1, of which 1 were waited for; matrix products, arithmetic and copies ran while one was open for 0% of the time, Pallas kernels for 0%

commit v1 on v0

v1 whole, which is shorter than its diff:
```python
import functools
import math

import jax
import jax.numpy as jnp
import numpy as np
from jax import lax
from jax.experimental import pallas as pl
from jax.experimental.pallas import tpu as pltpu
from jax.sharding import PartitionSpec as P

EPS = 1e-5
NEG = -1e30
F32 = jnp.float32
BF16 = jnp.bfloat16
MESH = pl.DeviceIdType.MESH
SLOTS = 6
GH = 8
KB = 512


def _gelu(x):
    return 0.5 * x * (1.0 + lax.erf(x * np.float32(math.sqrt(0.5))))


def _kernel(dims, x_hbm, g1_hbm, b1_hbm, g2_hbm, b2_hbm, inv_hbm, wqkv, wo, w1, w2, y_hbm,
            xall, gb, inv_v, a_v, m_v, h_v, aw, bw, sbuf, rbuf, obuf, orecv, ocat, yacc, yrecv, ybuf, cs,
            small_sem, a_sem, b_sem, xs_sem, xr_sem, qs_sem, qr_sem, os_sem, or_sem, ys_sem, yr_sem, loc_sem, out_sem):
    r, d, nh, dh, f, nchip = dims
    half = dh // 2
    dc = d // 2
    fc = f // 2
    cw = GH * dh
    ngrp = nchip // GH
    nm = fc // cw
    r2 = 2 * r
    s = lax.axis_index("seq")
    c = lax.rem(s, 2)
    me = lax.div(s, 2)
    partner = s + 1 - 2 * c

    def dev(chip):
        return {"seq": 2 * chip + c}

    barrier = pltpu.get_barrier_semaphore()
    pl.semaphore_signal(barrier, inc=1, device_id={"seq": partner}, device_id_type=MESH)
    for i in range(1, nchip):
        pl.semaphore_signal(barrier, inc=1, device_id=dev(lax.rem(me + i, nchip)), device_id_type=MESH)

    def qkv_copy(g, t):
        col = pl.multiple_of(t * d + c * dc + g * cw, 128)
        n = 3 * g + t
        return pltpu.make_async_copy(wqkv.at[:, pl.ds(col, cw)], aw.at[n], a_sem.at[n])

    def w1_copy(m):
        col = pl.multiple_of(c * fc + m * cw, 128)
        n = lax.rem(m, SLOTS)
        return pltpu.make_async_copy(w1.at[:, pl.ds(col, cw)], aw.at[n], a_sem.at[n])

    nb2 = nm
    nbo = dc // cw

    def b_copy(n):
        if n < nb2:
            return pltpu.make_async_copy(w2.at[pl.ds(pl.multiple_of(c * fc + n * cw, 128), cw), :],
                                         bw.at[pl.ds(n * cw, cw), :], b_sem.at[n])
        k = n - nb2
        return pltpu.make_async_copy(wo.at[pl.ds(pl.multiple_of(c * dc + k * cw, 128), cw), :],
                                     bw.at[pl.ds(n * cw, cw), :], b_sem.at[n])

    mine = pl.ds(pl.multiple_of(c * r, r), r)
    smalls = [
        pltpu.make_async_copy(x_hbm, xall.at[mine, :], small_sem.at[0]),
        pltpu.make_async_copy(g1_hbm, gb.at[0], small_sem.at[1]),
        pltpu.make_async_copy(b1_hbm, gb.at[1], small_sem.at[2]),
        pltpu.make_async_copy(g2_hbm, gb.at[2], small_sem.at[3]),
        pltpu.make_async_copy(b2_hbm, gb.at[3], small_sem.at[4]),
        pltpu.make_async_copy(inv_hbm, inv_v, small_sem.at[5]),
    ]
    for cp in smalls:
        cp.start()
    for g in range(ngrp):
        for t in range(3):
            qkv_copy(g, t).start()
    for n in range(2):
        b_copy(n).start()

    smalls[5].wait()
    pos = (me * r2 + lax.broadcasted_iota(jnp.int32, (r2, 128), 0)).astype(F32)
    ang = pos * inv_v[0:1, :]
    cos = jnp.cos(ang)
    sin = jnp.sin(ang)
    lane = lax.broadcasted_iota(jnp.int32, (r2, 128), 1)
    sin = jnp.where(lane < half, -sin, sin)
    cs[0] = jnp.concatenate([cos[:, :dh]] * GH, axis=1)
    cs[1] = jnp.concatenate([sin[:, :dh]] * GH, axis=1)

    for cp in smalls[:5]:
        cp.wait()
    pl.semaphore_wait(barrier, nchip)
    xcopy = pltpu.make_async_remote_copy(
        src_ref=xall.at[mine, :], dst_ref=xall.at[mine, :], send_sem=xs_sem, recv_sem=xr_sem,
        device_id={"seq": partner}, device_id_type=MESH)
    xcopy.start()
    xcopy.wait()

    xf = xall[...].astype(F32)
    mu = jnp.mean(xf, axis=-1, keepdims=True)
    xc = xf - mu
    var = jnp.mean(jnp.square(xc), axis=-1, keepdims=True)
    xn = xc * lax.rsqrt(var + EPS)
    a_v[...] = (xn * gb[0] + gb[1]).astype(BF16)
    m_v[...] = (xn * gb[2] + gb[3]).astype(BF16)

    lane_c = lax.rem(lax.broadcasted_iota(jnp.int32, (r2, cw), 1), dh)

    def rope(t):
        tf = t.astype(F32)
        up = pltpu.roll(tf, cw - half, axis=1)
        dn = pltpu.roll(tf, half, axis=1)
        rot = jnp.where(lane_c < half, up, dn)
        return (tf * cs[0] + rot * cs[1]).astype(BF16)

    def q_send(src, chip):
        return pltpu.make_async_remote_copy(
            src_ref=sbuf.at[chip], dst_ref=rbuf.at[pl.ds(pl.multiple_of(src * r2, r2), r2), :],
            send_sem=qs_sem.at[chip], recv_sem=qr_sem.at[src], device_id=dev(chip), device_id_type=MESH)

    def q_local():
        return pltpu.make_async_copy(
            sbuf.at[me], rbuf.at[pl.ds(pl.multiple_of(me * r2, r2), r2), :], loc_sem.at[0])

    for g in range(ngrp):
        parts = []
        for t in range(3):
            qkv_copy(g, t).wait()
            val = jnp.dot(a_v[...], aw[3 * g + t], preferred_element_type=F32).astype(BF16)
            w1_copy(3 * g + t).start()
            parts.append(rope(val) if t < 2 else val)
        for j in range(GH):
            sl = slice(j * dh, (j + 1) * dh)
            sbuf[g * GH + j] = jnp.concatenate(
                [parts[0][:, sl], parts[1][:, sl], parts[2][:, sl], jnp.zeros((r2, 256 - 3 * dh), BF16)], axis=1)

        def send(j, carry):
            chip = g * GH + lax.rem(j + me, GH)

            @pl.when(chip != me)
            def _():
                q_send(me, chip).start()

            @pl.when(chip == me)
            def _():
                q_local().start()
            return carry

        lax.fori_loop(0, GH, send, 0)

    def mlp1(m, carry):
        w1_copy(m).wait()
        t = jnp.dot(m_v[...], aw[lax.rem(m, SLOTS)], preferred_element_type=F32)
        h_v[:, pl.ds(pl.multiple_of(m * cw, 128), cw)] = _gelu(t).astype(BF16)

        @pl.when(m < nm - SLOTS)
        def _():
            w1_copy(m + SLOTS).start()
        return carry

    lax.fori_loop(0, nm - SLOTS, mlp1, 0)
    for n in range(2, nb2 + nbo):
        b_copy(n).start()
    lax.fori_loop(nm - SLOTS, nm, mlp1, 0)

    q_local().wait()

    def q_wait(i, carry):
        chip = lax.rem(me + i, nchip)
        q_send(chip, chip).wait()
        return carry

    lax.fori_loop(1, nchip, q_wait, 0)

    scale = dh ** -0.5
    qper = KB // r2

    def o_send(src, chip):
        return pltpu.make_async_remote_copy(
            src_ref=obuf.at[chip], dst_ref=orecv.at[src],
            send_sem=os_sem.at[chip], recv_sem=or_sem.at[src], device_id=dev(chip), device_id_type=MESH)

    def o_local():
        return pltpu.make_async_copy(obuf.at[me], orecv.at[me], loc_sem.at[1])

    def attend(i, carry):
        j = lax.rem(me + 1 + i, nchip)
        row0 = pl.multiple_of(j * r2, r2)

        def case(nk):
            kn = nk * KB
            q = rbuf[pl.ds(row0, r2), 0:128]
            lq = jnp.concatenate([jnp.zeros((r2, dh), BF16), q[:, :dh], jnp.zeros((r2, 256 - 2 * dh), BF16)], axis=1)
            sc = lax.dot_general(lq, rbuf[0:kn, :], (((1,), (1,)), ((), ())), preferred_element_type=F32) * scale
            last = sc[:, kn - KB:]
            rows = row0 + lax.broadcasted_iota(jnp.int32, (r2, KB), 0)
            cols = (kn - KB) + lax.broadcasted_iota(jnp.int32, (r2, KB), 1)
            last = jnp.where(cols <= rows, last, NEG)
            sc = last if nk == 1 else jnp.concatenate([sc[:, :kn - KB], last], axis=1)
            mx = jnp.max(sc, axis=-1, keepdims=True)
            e = jnp.exp(sc - mx)
            p = (e * (1.0 / jnp.sum(e, axis=-1, keepdims=True))).astype(BF16)
            o = jnp.dot(p, rbuf[0:kn, 128:256], preferred_element_type=F32)
            obuf[j] = pltpu.roll(o, 128 - (2 * dh - 128), axis=1).astype(BF16)

        for nk in range(1, nchip // qper + 1):
            pl.when(lax.div(j, qper) == nk - 1)(functools.partial(case, nk))

        @pl.when(j != me)
        def _():
            o_send(me, j).start()

        @pl.when(j == me)
        def _():
            o_local().start()
        return carry

    lax.fori_loop(0, nchip, attend, 0)

    for n in range(nb2):
        b_copy(n).wait()
    nt = 256

    def mlp2(n, carry):
        cols = pl.ds(pl.multiple_of(n * nt, 128), nt)
        t = jnp.dot(h_v[...], bw[0:fc, cols], preferred_element_type=F32)
        yacc[:, :, cols] = t.reshape(2, r, nt)
        return carry

    lax.fori_loop(0, d // nt, mlp2, 0)

    o_local().wait()

    def o_wait(i, carry):
        chip = lax.rem(me + i, nchip)
        o_send(chip, chip).wait()
        return carry

    lax.fori_loop(1, nchip, o_wait, 0)
    ocat[...] = jnp.concatenate([orecv[j][:, :dh] for j in range(nchip)], axis=1)
    for n in range(nb2, nb2 + nbo):
        b_copy(n).wait()

    ny = d // cw

    def y_send(n):
        cols = pl.ds(pl.multiple_of(n * cw, 128), cw)
        return pltpu.make_async_remote_copy(
            src_ref=yacc.at[1 - c, :, cols], dst_ref=yrecv.at[:, cols],
            send_sem=ys_sem.at[n], recv_sem=yr_sem.at[n], device_id={"seq": partner}, device_id_type=MESH)

    def proj(n, carry):
        cols = pl.ds(pl.multiple_of(n * cw, 128), cw)
        t = jnp.dot(ocat[...], bw[fc:fc + dc, cols], preferred_element_type=F32)
        yacc[:, :, cols] = yacc[:, :, cols] + t.reshape(2, r, cw)
        y_send(n).start()
        return carry

    lax.fori_loop(0, ny, proj, 0)

    def finish(n, carry):
        cols = pl.ds(pl.multiple_of(n * cw, 128), cw)
        y_send(n).wait()
        ybuf[:, cols] = (xall[mine, cols].astype(F32) + yacc[c, :, cols] + yrecv[:, cols]).astype(BF16)
        return carry

    lax.fori_loop(0, ny, finish, 0)
    out = pltpu.make_async_copy(ybuf, y_hbm, out_sem)
    out.start()
    out.wait()


def solution(mesh):
    nseq = mesh.shape["seq"]
    nchip = nseq // 2

    def local(x, g1, b1, g2, b2, wqkv, wo, w1, w2):
        r, d = x.shape
        nh, dh, _ = wo.shape
        f = w1.shape[1]
        if nh != nseq or nchip % GH or (KB % (2 * r)):
            raise ValueError("unsupported sizes")
        half = dh // 2
        inv = 10000.0 ** (-2.0 * np.arange(half) / dh)
        inv = np.concatenate([inv, inv, np.zeros(128 - dh)]).astype(np.float32)
        inv = jnp.asarray(np.tile(inv[None], (8, 1)))
        r2, cw, dc, fc = 2 * r, GH * dh, d // 2, f // 2
        nb = (fc + dc) // cw
        dma = pltpu.SemaphoreType.DMA
        flops = 2 * r2 * (d * 3 * dc + d * fc * 2 + dc * d)
        return pl.pallas_call(
            functools.partial(_kernel, (r, d, nh, dh, f, nchip)),
            out_shape=jax.ShapeDtypeStruct((r, d), BF16),
            in_specs=[pl.BlockSpec(memory_space=pl.ANY)] * 10,
            out_specs=pl.BlockSpec(memory_space=pl.ANY),
            scratch_shapes=[
                pltpu.VMEM((r2, d), BF16),
                pltpu.VMEM((4, 1, d), F32),
                pltpu.VMEM((8, 128), F32),
                pltpu.VMEM((r2, d), BF16),
                pltpu.VMEM((r2, d), BF16),
                pltpu.VMEM((r2, fc), BF16),
                pltpu.VMEM((SLOTS, d, cw), BF16),
                pltpu.VMEM((fc + dc, d), BF16),
                pltpu.VMEM((nchip, r2, 256), BF16),
                pltpu.VMEM((nchip * r2, 256), BF16),
                pltpu.VMEM((nchip, r2, 128), BF16),
                pltpu.VMEM((nchip, r2, 128), BF16),
                pltpu.VMEM((r2, dc), BF16),
                pltpu.VMEM((2, r, d), F32),
                pltpu.VMEM((r, d), F32),
                pltpu.VMEM((r, d), BF16),
                pltpu.VMEM((2, r2, cw), F32),
                dma((6,)), dma((SLOTS,)), dma((nb,)), dma, dma,
                dma((nchip,)), dma((nchip,)), dma((nchip,)), dma((nchip,)),
                dma((d // cw,)), dma((d // cw,)), dma((2,)), dma,
            ],
            compiler_params=pltpu.CompilerParams(
                collective_id=0, has_side_effects=True, vmem_limit_bytes=67043328),
            cost_estimate=pl.CostEstimate(flops=flops, bytes_accessed=2 * (d * 3 * dc + d * f + dc * d), transcendentals=0),
            name="layer",
        )(x, g1.reshape(1, d), b1.reshape(1, d), g2.reshape(1, d), b2.reshape(1, d), inv,
          wqkv, wo.reshape(nh * dh, d), w1, w2)

    rows = P(("data", "seq"), None)
    rep = P()
    return jax.shard_map(local, mesh=mesh,
                         in_specs=(rows, rep, rep, rep, rep, rep, rep, rep, rep),
                         out_specs=rows, check_vma=False)
```

time: 136 us -> 63.6 us (0.47)
  the two profiles are of different devices: /device:TPU:97 before, /device:TPU:121 now
where the time goes in v1:
time: 63.6 us; the launch traced here: 63.3 us
  Pallas kernels  56.3 us (89%)
  local copies, waits for them, and re-layouts  6.95 us (11%)
    pallas_call x1, Pallas kernels, local(): pl.pallas_call(functools.partial(_kernel, (r, d, nh, dh, f, nchip)), out_...  56.3 us
    unnamed x1, local copies, waits for them, and re-layouts  1.72 us
    reshape x1, local copies, waits for them, and re-layouts, local(): g1.reshape(1, d)  1.31 us
    reshape x1, local copies, waits for them, and re-layouts, local(): g2.reshape(1, d)  1.31 us
    reshape x1, local copies, waits for them, and re-layouts, local(): b2.reshape(1, d)  1.31 us
    reshape x1, local copies, waits for them, and re-layouts, local(): b1.reshape(1, d)  1.3 us

profile of v1, /device:TPU:121, one launch (start us, length us, event | category | flops | bytes accessed | tf_op | source)
XLA Modules:
  0.0 63.3 jit_solution(15966990068566616005)
XLA Ops:
  0.0 1.3 %reshape.15.g1_hbm = f32[1,2560]{1,0:T(1,128)} reshape(f32[2560]{0:T(1024)} %param.11) | data formatting | bytes 20480 | tf_op jit(solution)/shard_map/reshape | solution.py:330
  1.3 1.3 %reshape.16.b1_hbm = f32[1,2560]{1,0:T(1,128)} reshape(f32[2560]{0:T(1024)} %param.12) | data formatting | bytes 20480 | tf_op jit(solution)/shard_map/reshape | solution.py:330
  2.6 1.3 %reshape.17.g2_hbm = f32[1,2560]{1,0:T(1,128)} reshape(f32[2560]{0:T(1024)} %param.13) | data formatting | bytes 20480 | tf_op jit(solution)/shard_map/reshape | solution.py:330
  3.9 1.3 %reshape.18.b2_hbm = f32[1,2560]{1,0:T(1,128)} reshape(f32[2560]{0:T(1024)} %param.14) | data formatting | bytes 20480 | tf_op jit(solution)/shard_map/reshape | solution.py:330
  5.2 56.3 %layer.1 = bf16[64,2560]{1,0:T(8,128)(2,1)} custom-call(bf16[64,2560]{1,0:T(8,128)(2,1)} %x_hbm.1, f32[1,2560]{1,0:T(1,128)} %reshape.15.g1_hbm, f32[1,2560]{1,0:T(1,128)} %reshape.16.b1_hbm, f32[1,2560]{1,0:T(1,128)} %reshape.17.g2_hbm, f32[1,2560]{1,0:T(1,128)} %reshape.18.b2_hbm, f32[8,128]{1,0:T(8,128)} %constant.2.clone.inv_hbm, ...), custom_call_target="tpu_custom_call" | custom-call | flops 10066329600 | bytes 78643200 | tf_op jit(solution)/shard_map/layer/pallas_call | solution.py:299
  61.6 1.7 %copy.12 = bf16[64,2560]{1,0:T(8,128)(2,1)} copy(bf16[64,2560]{1,0:T(8,128)(2,1)} %layer.1) | data formatting | bytes 655360

commit v2 on v1

--- a/solution.py
+++ b/solution.py
@@ -24,7 +24,7 @@
 
 
 def _kernel(dims, x_hbm, g1_hbm, b1_hbm, g2_hbm, b2_hbm, inv_hbm, wqkv, wo, w1, w2, y_hbm,
-            xall, gb, inv_v, a_v, m_v, h_v, aw, bw, sbuf, rbuf, obuf, orecv, ocat, yacc, yrecv, ybuf, cs,
+            xall, g1_v, b1_v, g2_v, b2_v, inv_v, a_v, m_v, t_v, h_v, aw, bw, sbuf, rbuf, obuf, orecv, ocat, yacc, yrecv, ybuf, cs,
             small_sem, a_sem, b_sem, xs_sem, xr_sem, qs_sem, qr_sem, os_sem, or_sem, ys_sem, yr_sem, loc_sem, out_sem):
     r, d, nh, dh, f, nchip = dims
     half = dh // 2
@@ -42,13 +42,11 @@
     def dev(chip):
         return {"seq": 2 * chip + c}
 
-    barrier = pltpu.get_barrier_semaphore()
-    pl.semaphore_signal(barrier, inc=1, device_id={"seq": partner}, device_id_type=MESH)
-    for i in range(1, nchip):
-        pl.semaphore_signal(barrier, inc=1, device_id=dev(lax.rem(me + i, nchip)), device_id_type=MESH)
+    def group(g):
+        return lax.rem(g + lax.div(2 * me, nchip) + 1, ngrp)
 
     def qkv_copy(g, t):
-        col = pl.multiple_of(t * d + c * dc + g * cw, 128)
+        col = pl.multiple_of(t * d + c * dc + group(g) * cw, 128)
         n = 3 * g + t
         return pltpu.make_async_copy(wqkv.at[:, pl.ds(col, cw)], aw.at[n], a_sem.at[n])
 
@@ -68,13 +66,12 @@
         return pltpu.make_async_copy(wo.at[pl.ds(pl.multiple_of(c * dc + k * cw, 128), cw), :],
                                      bw.at[pl.ds(n * cw, cw), :], b_sem.at[n])
 
-    mine = pl.ds(pl.multiple_of(c * r, r), r)
     smalls = [
-        pltpu.make_async_copy(x_hbm, xall.at[mine, :], small_sem.at[0]),
-        pltpu.make_async_copy(g1_hbm, gb.at[0], small_sem.at[1]),
-        pltpu.make_async_copy(b1_hbm, gb.at[1], small_sem.at[2]),
-        pltpu.make_async_copy(g2_hbm, gb.at[2], small_sem.at[3]),
-        pltpu.make_async_copy(b2_hbm, gb.at[3], small_sem.at[4]),
+        pltpu.make_async_copy(x_hbm, xall.at[c], small_sem.at[0]),
+        pltpu.make_async_copy(g1_hbm, g1_v, small_sem.at[1]),
+        pltpu.make_async_copy(b1_hbm, b1_v, small_sem.at[2]),
+        pltpu.make_async_copy(g2_hbm, g2_v, small_sem.at[3]),
+        pltpu.make_async_copy(b2_hbm, b2_v, small_sem.at[4]),
         pltpu.make_async_copy(inv_hbm, inv_v, small_sem.at[5]),
     ]
     for cp in smalls:
@@ -85,7 +82,13 @@
     for n in range(2):
         b_copy(n).start()
 
-    smalls[5].wait()
+    barrier = pltpu.get_barrier_semaphore()
+    pl.semaphore_signal(barrier, inc=1, device_id={"seq": partner}, device_id_type=MESH)
+    for i in range(1, nchip):
+        pl.semaphore_signal(barrier, inc=1, device_id=dev(lax.rem(me + i, nchip)), device_id_type=MESH)
+
+    for cp in smalls:
+        cp.wait()
     pos = (me * r2 + lax.broadcasted_iota(jnp.int32, (r2, 128), 0)).astype(F32)
     ang = pos * inv_v[0:1, :]
     cos = jnp.cos(ang)
@@ -95,22 +98,24 @@
     cs[0] = jnp.concatenate([cos[:, :dh]] * GH, axis=1)
     cs[1] = jnp.concatenate([sin[:, :dh]] * GH, axis=1)
 
-    for cp in smalls[:5]:
-        cp.wait()
+    def norms(which):
+        xf = xall[which].astype(F32)
+        mu = jnp.mean(xf, axis=-1, keepdims=True)
+        xc = xf - mu
+        var = jnp.mean(jnp.square(xc), axis=-1, keepdims=True)
+        xn = xc * lax.rsqrt(var + EPS)
+        a_v[which] = (xn * g1_v[...].reshape(1, d) + b1_v[...].reshape(1, d)).astype(BF16)
+        m_v[which] = (xn * g2_v[...].reshape(1, d) + b2_v[...].reshape(1, d)).astype(BF16)
+
+    norms(c)
+
     pl.semaphore_wait(barrier, nchip)
     xcopy = pltpu.make_async_remote_copy(
-        src_ref=xall.at[mine, :], dst_ref=xall.at[mine, :], send_sem=xs_sem, recv_sem=xr_sem,
+        src_ref=xall.at[c], dst_ref=xall.at[c], send_sem=xs_sem, recv_sem=xr_sem,
         device_id={"seq": partner}, device_id_type=MESH)
     xcopy.start()
     xcopy.wait()
-
-    xf = xall[...].astype(F32)
-    mu = jnp.mean(xf, axis=-1, keepdims=True)
-    xc = xf - mu
-    var = jnp.mean(jnp.square(xc), axis=-1, keepdims=True)
-    xn = xc * lax.rsqrt(var + EPS)
-    a_v[...] = (xn * gb[0] + gb[1]).astype(BF16)
-    m_v[...] = (xn * gb[2] + gb[3]).astype(BF16)
+    norms(1 - c)
 
     lane_c = lax.rem(lax.broadcasted_iota(jnp.int32, (r2, cw), 1), dh)
 
@@ -131,19 +136,21 @@
             sbuf.at[me], rbuf.at[pl.ds(pl.multiple_of(me * r2, r2), r2), :], loc_sem.at[0])
 
     for g in range(ngrp):
-        parts = []
+        gg = group(g)
         for t in range(3):
             qkv_copy(g, t).wait()
-            val = jnp.dot(a_v[...], aw[3 * g + t], preferred_element_type=F32).astype(BF16)
-            w1_copy(3 * g + t).start()
-            parts.append(rope(val) if t < 2 else val)
+        a = a_v[...].reshape(r2, d)
+        parts = [jnp.dot(a, aw[3 * g + t], preferred_element_type=F32).astype(BF16) for t in range(3)]
+        parts = [rope(parts[0]), rope(parts[1]), parts[2]]
         for j in range(GH):
             sl = slice(j * dh, (j + 1) * dh)
-            sbuf[g * GH + j] = jnp.concatenate(
+            sbuf[gg * GH + j] = jnp.concatenate(
                 [parts[0][:, sl], parts[1][:, sl], parts[2][:, sl], jnp.zeros((r2, 256 - 3 * dh), BF16)], axis=1)
+        for t in range(3):
+            w1_copy(3 * g + t).start()
 
         def send(j, carry):
-            chip = g * GH + lax.rem(j + me, GH)
+            chip = gg * GH + lax.rem(j + me, GH)
 
             @pl.when(chip != me)
             def _():
@@ -156,20 +163,47 @@
 
         lax.fori_loop(0, GH, send, 0)
 
+    def up(m):
+        t_v[lax.rem(m, 2)] = jnp.dot(m_v[...].reshape(r2, d), aw[lax.rem(m, SLOTS)], preferred_element_type=F32)
+
+    def act(m):
+        h_v[:, pl.ds(pl.multiple_of(m * cw, 128), cw)] = _gelu(t_v[lax.rem(m, 2)]).astype(BF16)
+
+    w1_copy(0).wait()
+    up(0)
+    w1_copy(SLOTS).start()
+
     def mlp1(m, carry):
         w1_copy(m).wait()
-        t = jnp.dot(m_v[...], aw[lax.rem(m, SLOTS)], preferred_element_type=F32)
-        h_v[:, pl.ds(pl.multiple_of(m * cw, 128), cw)] = _gelu(t).astype(BF16)
+        up(m)
+        act(m - 1)
 
         @pl.when(m < nm - SLOTS)
         def _():
             w1_copy(m + SLOTS).start()
         return carry
 
-    lax.fori_loop(0, nm - SLOTS, mlp1, 0)
+    lax.fori_loop(1, nm - SLOTS, mlp1, 0)
     for n in range(2, nb2 + nbo):
         b_copy(n).start()
     lax.fori_loop(nm - SLOTS, nm, mlp1, 0)
+    act(nm - 1)
+
+    nt = 256
+    early = nb2 // 2
+
+    def down(k0, k1, first):
+        def body(n, carry):
+            cols = pl.ds(pl.multiple_of(n * nt, 128), nt)
+            t = jnp.dot(h_v[:, k0:k1], bw[k0:k1, cols], preferred_element_type=F32).reshape(2, r, nt)
+            yacc[:, :, cols] = t if first else yacc[:, :, cols] + t
+            return carry
+
+        lax.fori_loop(0, d // nt, body, 0)
+
+    for n in range(early):
+        b_copy(n).wait()
+    down(0, early * cw, True)
 
     q_local().wait()
 
@@ -191,51 +225,59 @@
     def o_local():
         return pltpu.make_async_copy(obuf.at[me], orecv.at[me], loc_sem.at[1])
 
+    nq = nchip // qper
+    og = r2 // 16
+
     def attend(i, carry):
-        j = lax.rem(me + 1 + i, nchip)
-        row0 = pl.multiple_of(j * r2, r2)
-
-        def case(nk):
-            kn = nk * KB
-            q = rbuf[pl.ds(row0, r2), 0:128]
-            lq = jnp.concatenate([jnp.zeros((r2, dh), BF16), q[:, :dh], jnp.zeros((r2, 256 - 2 * dh), BF16)], axis=1)
-            sc = lax.dot_general(lq, rbuf[0:kn, :], (((1,), (1,)), ((), ())), preferred_element_type=F32) * scale
-            last = sc[:, kn - KB:]
-            rows = row0 + lax.broadcasted_iota(jnp.int32, (r2, KB), 0)
-            cols = (kn - KB) + lax.broadcasted_iota(jnp.int32, (r2, KB), 1)
-            last = jnp.where(cols <= rows, last, NEG)
-            sc = last if nk == 1 else jnp.concatenate([sc[:, :kn - KB], last], axis=1)
-            mx = jnp.max(sc, axis=-1, keepdims=True)
-            e = jnp.exp(sc - mx)
-            p = (e * (1.0 / jnp.sum(e, axis=-1, keepdims=True))).astype(BF16)
-            o = jnp.dot(p, rbuf[0:kn, 128:256], preferred_element_type=F32)
-            obuf[j] = pltpu.roll(o, 128 - (2 * dh - 128), axis=1).astype(BF16)
-
-        for nk in range(1, nchip // qper + 1):
-            pl.when(lax.div(j, qper) == nk - 1)(functools.partial(case, nk))
-
-        @pl.when(j != me)
-        def _():
-            o_send(me, j).start()
-
-        @pl.when(j == me)
-        def _():
-            o_local().start()
-        return carry
-
-    lax.fori_loop(0, nchip, attend, 0)
-
-    for n in range(nb2):
+        u = lax.rem(me + i, qper)
+        blocks = [qper * n + u for n in range(nq)]
+        row0 = [pl.multiple_of(j * r2, r2) for j in blocks]
+        lq = []
+        for n in range(nq):
+            q = rbuf[pl.ds(row0[n], r2), 0:128]
+            lq.append(jnp.concatenate(
+                [jnp.zeros((r2, dh), BF16), q[:, :dh], jnp.zeros((r2, 256 - 2 * dh), BF16)], axis=1))
+        rows = u * r2 + lax.broadcasted_iota(jnp.int32, (r2, KB), 0)
+        cols = lax.broadcasted_iota(jnp.int32, (r2, KB), 1)
+        seen = cols <= rows
+        sc = [[] for _ in range(nq)]
+        for k in range(nq):
+            t = lax.dot_general(jnp.concatenate(lq[k:], axis=0), rbuf[k * KB:(k + 1) * KB, :],
+                                (((1,), (1,)), ((), ())), preferred_element_type=F32)
+            for n in range(k, nq):
+                tn = t[(n - k) * r2:(n - k + 1) * r2]
+                sc[n].append(jnp.where(seen, tn, NEG) if n == k else tn)
+        for n in range(nq):
+            mx = functools.reduce(jnp.maximum, sc[n])
+            mx = jnp.max(mx, axis=-1, keepdims=True)
+            e = [jnp.exp((t - mx) * scale) for t in sc[n]]
+            inv_l = 1.0 / jnp.sum(functools.reduce(jnp.add, e), axis=-1, keepdims=True)
+            p = jnp.concatenate([(t * inv_l).astype(BF16) for t in e], axis=1)
+            o = jnp.dot(p, rbuf[0:(n + 1) * KB, 128:256], preferred_element_type=F32)
+            v0 = 2 * dh - 128
+            obuf[blocks[n]] = jnp.concatenate(
+                [o[16 * g:16 * (g + 1), v0:v0 + dh] for g in range(og)], axis=1).astype(BF16)
+
+        def send(n, carry):
+            j = qper * n + u
+
+            @pl.when(j != me)
+            def _():
+                o_send(me, j).start()
+
+            @pl.when(j == me)
+            def _():
+                o_local().start()
+            return carry
+
+        lax.fori_loop(0, nq, send, 0)
+        return carry
+
+    lax.fori_loop(0, qper, attend, 0)
+
+    for n in range(early, nb2):
         b_copy(n).wait()
-    nt = 256
-
-    def mlp2(n, carry):
-        cols = pl.ds(pl.multiple_of(n * nt, 128), nt)
-        t = jnp.dot(h_v[...], bw[0:fc, cols], preferred_element_type=F32)
-        yacc[:, :, cols] = t.reshape(2, r, nt)
-        return carry
-
-    lax.fori_loop(0, d // nt, mlp2, 0)
+    down(early * cw, fc, False)
 
     o_local().wait()
 
@@ -245,7 +287,9 @@
         return carry
 
     lax.fori_loop(1, nchip, o_wait, 0)
-    ocat[...] = jnp.concatenate([orecv[j][:, :dh] for j in range(nchip)], axis=1)
+    for g in range(og):
+        ocat[16 * g:16 * (g + 1), :] = jnp.concatenate(
+            [orecv[j][:, g * dh:(g + 1) * dh] for j in range(nchip)], axis=1)
     for n in range(nb2, nb2 + nbo):
         b_copy(n).wait()
 
@@ -269,7 +313,7 @@
     def finish(n, carry):
         cols = pl.ds(pl.multiple_of(n * cw, 128), cw)
         y_send(n).wait()
-        ybuf[:, cols] = (xall[mine, cols].astype(F32) + yacc[c, :, cols] + yrecv[:, cols]).astype(BF16)
+        ybuf[:, cols] = (xall[c, :, cols].astype(F32) + yacc[c, :, cols] + yrecv[:, cols]).astype(BF16)
         return carry
 
     lax.fori_loop(0, ny, finish, 0)
@@ -302,18 +346,22 @@
             in_specs=[pl.BlockSpec(memory_space=pl.ANY)] * 10,
             out_specs=pl.BlockSpec(memory_space=pl.ANY),
             scratch_shapes=[
-                pltpu.VMEM((r2, d), BF16),
-                pltpu.VMEM((4, 1, d), F32),
+                pltpu.VMEM((2, r, d), BF16),
+                pltpu.VMEM((d,), F32),
+                pltpu.VMEM((d,), F32),
+                pltpu.VMEM((d,), F32),
+                pltpu.VMEM((d,), F32),
                 pltpu.VMEM((8, 128), F32),
-                pltpu.VMEM((r2, d), BF16),
-                pltpu.VMEM((r2, d), BF16),
+                pltpu.VMEM((2, r, d), BF16),
+                pltpu.VMEM((2, r, d), BF16),
+                pltpu.VMEM((2, r2, cw), F32),
                 pltpu.VMEM((r2, fc), BF16),
                 pltpu.VMEM((SLOTS, d, cw), BF16),
                 pltpu.VMEM((fc + dc, d), BF16),
                 pltpu.VMEM((nchip, r2, 256), BF16),
                 pltpu.VMEM((nchip * r2, 256), BF16),
-                pltpu.VMEM((nchip, r2, 128), BF16),
-                pltpu.VMEM((nchip, r2, 128), BF16),
+                pltpu.VMEM((nchip, 16, r2 // 16 * dh), BF16),
+                pltpu.VMEM((nchip, 16, r2 // 16 * dh), BF16),
                 pltpu.VMEM((r2, dc), BF16),
                 pltpu.VMEM((2, r, d), F32),
                 pltpu.VMEM((r, d), F32),
@@ -327,7 +375,7 @@
                 collective_id=0, has_side_effects=True, vmem_limit_bytes=67043328),
             cost_estimate=pl.CostEstimate(flops=flops, bytes_accessed=2 * (d * 3 * dc + d * f + dc * d), transcendentals=0),
             name="layer",
-        )(x, g1.reshape(1, d), b1.reshape(1, d), g2.reshape(1, d), b2.reshape(1, d), inv,
+        )(x, g1, b1, g2, b2, inv,
           wqkv, wo.reshape(nh * dh, d), w1, w2)
 
     rows = P(("data", "seq"), None)

time: 63.6 us -> 52.9 us (0.83)
  the two profiles are of different devices: /device:TPU:121 before, /device:TPU:97 now
where the time goes in v2:
time: 52.9 us; the launch traced here: 52.8 us
  Pallas kernels  51.1 us (97%)
  local copies, waits for them, and re-layouts  1.72 us (3%)
    pallas_call x1, Pallas kernels, local(): pl.pallas_call(functools.partial(_kernel, (r, d, nh, dh, f, nchip)), out_...  51.1 us
    unnamed x1, local copies, waits for them, and re-layouts  1.72 us

profile of v2, /device:TPU:97, one launch (start us, length us, event | category | flops | bytes accessed | tf_op | source)
XLA Modules:
  0.0 52.8 jit_solution(6175569908169890281)
XLA Ops:
  0.0 51.1 %layer.1 = bf16[64,2560]{1,0:T(8,128)(2,1)} custom-call(bf16[64,2560]{1,0:T(8,128)(2,1)} %x_hbm.1, f32[2560]{0:T(1024)} %g1_hbm.1, f32[2560]{0:T(1024)} %b1_hbm.1, f32[2560]{0:T(1024)} %g2_hbm.1, f32[2560]{0:T(1024)} %b2_hbm.1, f32[8,128]{1,0:T(8,128)} %constant.2.clone.inv_hbm, bf16[2560,7680]{1,0:T(8,128)(2,1)} %wqkv.1, bf16[2560,2560]{1,0:T(8,128)(2,1)} %bitcast.1, ...), custom_call_target="tpu_custom_call" | custom-call | flops 10066329600 | bytes 78643200 | tf_op jit(solution)/shard_map/layer/pallas_call | solution.py:343
  51.1 1.7 %copy.12 = bf16[64,2560]{1,0:T(8,128)(2,1)} copy(bf16[64,2560]{1,0:T(8,128)(2,1)} %layer.1) | data formatting | bytes 655360

commit v3 on v2

--- a/solution.py
+++ b/solution.py
@@ -42,8 +42,11 @@
     def dev(chip):
         return {"seq": 2 * chip + c}
 
+    def owner(g, j):
+        return ngrp * j + (j // 2 + g) % ngrp
+
     def group(g):
-        return lax.rem(g + lax.div(2 * me, nchip) + 1, ngrp)
+        return (me % ngrp + me // (2 * ngrp) + g + 1) % ngrp
 
     def qkv_copy(g, t):
         col = pl.multiple_of(t * d + c * dc + group(g) * cw, 128)
@@ -78,25 +81,14 @@
         cp.start()
     for g in range(ngrp):
         for t in range(3):
-            qkv_copy(g, t).start()
+            qkv_copy(g, t).start(priority=1)
     for n in range(2):
-        b_copy(n).start()
+        b_copy(n).start(priority=1)
 
     barrier = pltpu.get_barrier_semaphore()
     pl.semaphore_signal(barrier, inc=1, device_id={"seq": partner}, device_id_type=MESH)
     for i in range(1, nchip):
         pl.semaphore_signal(barrier, inc=1, device_id=dev(lax.rem(me + i, nchip)), device_id_type=MESH)
-
-    for cp in smalls:
-        cp.wait()
-    pos = (me * r2 + lax.broadcasted_iota(jnp.int32, (r2, 128), 0)).astype(F32)
-    ang = pos * inv_v[0:1, :]
-    cos = jnp.cos(ang)
-    sin = jnp.sin(ang)
-    lane = lax.broadcasted_iota(jnp.int32, (r2, 128), 1)
-    sin = jnp.where(lane < half, -sin, sin)
-    cs[0] = jnp.concatenate([cos[:, :dh]] * GH, axis=1)
-    cs[1] = jnp.concatenate([sin[:, :dh]] * GH, axis=1)
 
     def norms(which):
         xf = xall[which].astype(F32)
@@ -107,61 +99,104 @@
         a_v[which] = (xn * g1_v[...].reshape(1, d) + b1_v[...].reshape(1, d)).astype(BF16)
         m_v[which] = (xn * g2_v[...].reshape(1, d) + b2_v[...].reshape(1, d)).astype(BF16)
 
+    for cp in smalls[:5]:
+        cp.wait()
     norms(c)
 
+    smalls[5].wait()
+    pos = (me * r2 + lax.broadcasted_iota(jnp.int32, (r2, 128), 0)).astype(F32)
+    ang = pos * inv_v[0:1, :]
+    cos = jnp.cos(ang)
+    sin = jnp.sin(ang)
+    lane = lax.broadcasted_iota(jnp.int32, (r2, 128), 1)
+    sin = jnp.where(lane < half, -sin, sin)
+    cs[0] = jnp.concatenate([cos[:, :dh]] * GH, axis=1).reshape(2, r, cw)
+    cs[1] = jnp.concatenate([sin[:, :dh]] * GH, axis=1).reshape(2, r, cw)
+
+    lane_c = lax.rem(lax.broadcasted_iota(jnp.int32, (r, cw), 1), dh)
+
+    def rope(t, which):
+        tf = t.astype(F32)
+        up = pltpu.roll(tf, cw - half, axis=1)
+        dn = pltpu.roll(tf, half, axis=1)
+        rot = jnp.where(lane_c < half, up, dn)
+        return (tf * cs[0, which] + rot * cs[1, which]).astype(BF16)
+
+    def q_send(src, chip, which):
+        return pltpu.make_async_remote_copy(
+            src_ref=sbuf.at[chip, which], dst_ref=rbuf.at[pl.ds(pl.multiple_of(src * r2 + which * r, r), r), :],
+            send_sem=qs_sem.at[which, chip], recv_sem=qr_sem.at[which, src], device_id=dev(chip), device_id_type=MESH)
+
+    def q_local(which):
+        return pltpu.make_async_copy(
+            sbuf.at[me, which], rbuf.at[pl.ds(pl.multiple_of(me * r2 + which * r, r), r), :], loc_sem.at[which])
+
+    def q_part(g, which, t):
+        part = jnp.dot(a_v[which], aw[3 * g + t], preferred_element_type=F32).astype(BF16)
+        return rope(part, which) if t < 2 else part
+
+    def q_pack(which, gg, parts):
+        for j in range(GH):
+            sl = slice(j * dh, (j + 1) * dh)
+            sbuf[owner(gg, j), which] = jnp.concatenate(
+                [parts[0][:, sl], parts[1][:, sl], parts[2][:, sl], jnp.zeros((r, 256 - 3 * dh), BF16)], axis=1)
+
+    def q_group(g, gg):
+        a = a_v[...].reshape(r2, d)
+        parts = [jnp.dot(a, aw[3 * g + t], preferred_element_type=F32).astype(BF16) for t in range(3)]
+        for which in range(2):
+            pw = [p[which * r:(which + 1) * r] for p in parts]
+            pw = [rope(pw[0], which), rope(pw[1], which), pw[2]]
+            for j in range(GH):
+                sl = slice(j * dh, (j + 1) * dh)
+                sbuf[owner(gg, j), which] = jnp.concatenate(
+                    [pw[0][:, sl], pw[1][:, sl], pw[2][:, sl], jnp.zeros((r, 256 - 3 * dh), BF16)], axis=1)
+
+    def q_sends(gg, halves):
+        def send(j, carry):
+            chip = owner(gg, lax.rem(j + me // ngrp, GH))
+
+            @pl.when(chip != me)
+            def _():
+                for which in halves:
+                    q_send(me, chip, which).start()
+
+            @pl.when(chip == me)
+            def _():
+                for which in halves:
+                    q_local(which).start()
+            return carry
+
+        lax.fori_loop(0, GH, send, 0)
+
+    parts = []
+    qkv_copy(0, 0).wait()
+    parts.append(q_part(0, c, 0))
     pl.semaphore_wait(barrier, nchip)
     xcopy = pltpu.make_async_remote_copy(
         src_ref=xall.at[c], dst_ref=xall.at[c], send_sem=xs_sem, recv_sem=xr_sem,
         device_id={"seq": partner}, device_id_type=MESH)
     xcopy.start()
+
+    qkv_copy(0, 1).wait()
+    parts.append(q_part(0, c, 1))
+    qkv_copy(0, 2).wait()
+    parts.append(q_part(0, c, 2))
+    q_pack(c, group(0), parts)
+    q_sends(group(0), [c])
     xcopy.wait()
     norms(1 - c)
-
-    lane_c = lax.rem(lax.broadcasted_iota(jnp.int32, (r2, cw), 1), dh)
-
-    def rope(t):
-        tf = t.astype(F32)
-        up = pltpu.roll(tf, cw - half, axis=1)
-        dn = pltpu.roll(tf, half, axis=1)
-        rot = jnp.where(lane_c < half, up, dn)
-        return (tf * cs[0] + rot * cs[1]).astype(BF16)
-
-    def q_send(src, chip):
-        return pltpu.make_async_remote_copy(
-            src_ref=sbuf.at[chip], dst_ref=rbuf.at[pl.ds(pl.multiple_of(src * r2, r2), r2), :],
-            send_sem=qs_sem.at[chip], recv_sem=qr_sem.at[src], device_id=dev(chip), device_id_type=MESH)
-
-    def q_local():
-        return pltpu.make_async_copy(
-            sbuf.at[me], rbuf.at[pl.ds(pl.multiple_of(me * r2, r2), r2), :], loc_sem.at[0])
-
-    for g in range(ngrp):
-        gg = group(g)
+    q_pack(1 - c, group(0), [q_part(0, 1 - c, t) for t in range(3)])
+    for t in range(3):
+        w1_copy(t).start(priority=1)
+    q_sends(group(0), [1 - c])
+    for g in range(1, ngrp):
         for t in range(3):
             qkv_copy(g, t).wait()
-        a = a_v[...].reshape(r2, d)
-        parts = [jnp.dot(a, aw[3 * g + t], preferred_element_type=F32).astype(BF16) for t in range(3)]
-        parts = [rope(parts[0]), rope(parts[1]), parts[2]]
-        for j in range(GH):
-            sl = slice(j * dh, (j + 1) * dh)
-            sbuf[gg * GH + j] = jnp.concatenate(
-                [parts[0][:, sl], parts[1][:, sl], parts[2][:, sl], jnp.zeros((r2, 256 - 3 * dh), BF16)], axis=1)
+        q_group(g, group(g))
         for t in range(3):
-            w1_copy(3 * g + t).start()
-
-        def send(j, carry):
-            chip = gg * GH + lax.rem(j + me, GH)
-
-            @pl.when(chip != me)
-            def _():
-                q_send(me, chip).start()
-
-            @pl.when(chip == me)
-            def _():
-                q_local().start()
-            return carry
-
-        lax.fori_loop(0, GH, send, 0)
+            w1_copy(3 * g + t).start(priority=1)
+        q_sends(group(g), [0, 1])
 
     def up(m):
         t_v[lax.rem(m, 2)] = jnp.dot(m_v[...].reshape(r2, d), aw[lax.rem(m, SLOTS)], preferred_element_type=F32)
@@ -171,26 +206,24 @@
 
     w1_copy(0).wait()
     up(0)
-    w1_copy(SLOTS).start()
-
-    def mlp1(m, carry):
+    w1_copy(SLOTS).start(priority=1)
+
+    def mlp1(refill, m, carry):
         w1_copy(m).wait()
+        act(m - 1)
         up(m)
-        act(m - 1)
-
-        @pl.when(m < nm - SLOTS)
-        def _():
-            w1_copy(m + SLOTS).start()
-        return carry
-
-    lax.fori_loop(1, nm - SLOTS, mlp1, 0)
+        if refill:
+            w1_copy(m + SLOTS).start(priority=1)
+        return carry
+
+    lax.fori_loop(1, nm - SLOTS, functools.partial(mlp1, True), 0)
     for n in range(2, nb2 + nbo):
-        b_copy(n).start()
-    lax.fori_loop(nm - SLOTS, nm, mlp1, 0)
+        b_copy(n).start(priority=1)
+    lax.fori_loop(nm - SLOTS, nm, functools.partial(mlp1, False), 0)
     act(nm - 1)
 
-    nt = 256
-    early = nb2 // 2
+    nt = d // 2
+    early = 2
 
     def down(k0, k1, first):
         def body(n, carry):
@@ -205,16 +238,18 @@
         b_copy(n).wait()
     down(0, early * cw, True)
 
-    q_local().wait()
+    q_local(0).wait()
+    q_local(1).wait()
 
     def q_wait(i, carry):
         chip = lax.rem(me + i, nchip)
-        q_send(chip, chip).wait()
+        q_send(chip, chip, 0).wait()
+        q_send(chip, chip, 1).wait()
         return carry
 
     lax.fori_loop(1, nchip, q_wait, 0)
 
-    scale = dh ** -0.5
+    scale = dh ** -0.5 * math.log2(math.e)
     qper = KB // r2
 
     def o_send(src, chip):
@@ -223,34 +258,32 @@
             send_sem=os_sem.at[chip], recv_sem=or_sem.at[src], device_id=dev(chip), device_id_type=MESH)
 
     def o_local():
-        return pltpu.make_async_copy(obuf.at[me], orecv.at[me], loc_sem.at[1])
+        return pltpu.make_async_copy(obuf.at[me], orecv.at[me], loc_sem.at[2])
 
     nq = nchip // qper
     og = r2 // 16
 
     def attend(i, carry):
-        u = lax.rem(me + i, qper)
-        blocks = [qper * n + u for n in range(nq)]
+        us = [lax.rem(me + i + n, qper) for n in range(nq)]
+        blocks = [qper * n + us[n] for n in range(nq)]
         row0 = [pl.multiple_of(j * r2, r2) for j in blocks]
         lq = []
         for n in range(nq):
             q = rbuf[pl.ds(row0[n], r2), 0:128]
             lq.append(jnp.concatenate(
                 [jnp.zeros((r2, dh), BF16), q[:, :dh], jnp.zeros((r2, 256 - 2 * dh), BF16)], axis=1))
-        rows = u * r2 + lax.broadcasted_iota(jnp.int32, (r2, KB), 0)
-        cols = lax.broadcasted_iota(jnp.int32, (r2, KB), 1)
-        seen = cols <= rows
+        ahead = lax.broadcasted_iota(jnp.int32, (r2, KB), 1) - lax.broadcasted_iota(jnp.int32, (r2, KB), 0)
         sc = [[] for _ in range(nq)]
         for k in range(nq):
             t = lax.dot_general(jnp.concatenate(lq[k:], axis=0), rbuf[k * KB:(k + 1) * KB, :],
                                 (((1,), (1,)), ((), ())), preferred_element_type=F32)
             for n in range(k, nq):
                 tn = t[(n - k) * r2:(n - k + 1) * r2]
-                sc[n].append(jnp.where(seen, tn, NEG) if n == k else tn)
+                sc[n].append(jnp.where(ahead <= us[n] * r2, tn, NEG) if n == k else tn)
         for n in range(nq):
             mx = functools.reduce(jnp.maximum, sc[n])
             mx = jnp.max(mx, axis=-1, keepdims=True)
-            e = [jnp.exp((t - mx) * scale) for t in sc[n]]
+            e = [jnp.exp2((t - mx) * scale) for t in sc[n]]
             inv_l = 1.0 / jnp.sum(functools.reduce(jnp.add, e), axis=-1, keepdims=True)
             p = jnp.concatenate([(t * inv_l).astype(BF16) for t in e], axis=1)
             o = jnp.dot(p, rbuf[0:(n + 1) * KB, 128:256], preferred_element_type=F32)
@@ -259,7 +292,7 @@
                 [o[16 * g:16 * (g + 1), v0:v0 + dh] for g in range(og)], axis=1).astype(BF16)
 
         def send(n, carry):
-            j = qper * n + u
+            j = qper * n + lax.rem(me + i + n, qper)
 
             @pl.when(j != me)
             def _():
@@ -289,37 +322,42 @@
     lax.fori_loop(1, nchip, o_wait, 0)
     for g in range(og):
         ocat[16 * g:16 * (g + 1), :] = jnp.concatenate(
-            [orecv[j][:, g * dh:(g + 1) * dh] for j in range(nchip)], axis=1)
+            [orecv[owner(j // GH, j % GH)][:, g * dh:(g + 1) * dh] for j in range(nchip)], axis=1)
     for n in range(nb2, nb2 + nbo):
         b_copy(n).wait()
 
-    ny = d // cw
+    ny = 2
+    yw = d // ny
 
     def y_send(n):
-        cols = pl.ds(pl.multiple_of(n * cw, 128), cw)
+        cols = pl.ds(pl.multiple_of(n * yw, 128), yw)
         return pltpu.make_async_remote_copy(
             src_ref=yacc.at[1 - c, :, cols], dst_ref=yrecv.at[:, cols],
             send_sem=ys_sem.at[n], recv_sem=yr_sem.at[n], device_id={"seq": partner}, device_id_type=MESH)
 
     def proj(n, carry):
-        cols = pl.ds(pl.multiple_of(n * cw, 128), cw)
+        cols = pl.ds(pl.multiple_of(n * yw, 128), yw)
         t = jnp.dot(ocat[...], bw[fc:fc + dc, cols], preferred_element_type=F32)
-        yacc[:, :, cols] = yacc[:, :, cols] + t.reshape(2, r, cw)
+        yacc[:, :, cols] = yacc[:, :, cols] + t.reshape(2, r, yw)
         y_send(n).start()
         return carry
 
     lax.fori_loop(0, ny, proj, 0)
 
+    def y_out(n):
+        cols = pl.ds(pl.multiple_of(n * yw, 128), yw)
+        return pltpu.make_async_copy(ybuf.at[:, cols], y_hbm.at[:, cols], out_sem.at[n])
+
     def finish(n, carry):
-        cols = pl.ds(pl.multiple_of(n * cw, 128), cw)
+        cols = pl.ds(pl.multiple_of(n * yw, 128), yw)
         y_send(n).wait()
         ybuf[:, cols] = (xall[c, :, cols].astype(F32) + yacc[c, :, cols] + yrecv[:, cols]).astype(BF16)
+        y_out(n).start()
         return carry
 
     lax.fori_loop(0, ny, finish, 0)
-    out = pltpu.make_async_copy(ybuf, y_hbm, out_sem)
-    out.start()
-    out.wait()
+    for n in range(ny):
+        y_out(n).wait()
 
 
 def solution(mesh):
@@ -358,7 +396,7 @@
                 pltpu.VMEM((r2, fc), BF16),
                 pltpu.VMEM((SLOTS, d, cw), BF16),
                 pltpu.VMEM((fc + dc, d), BF16),
-                pltpu.VMEM((nchip, r2, 256), BF16),
+                pltpu.VMEM((nchip, 2, r, 256), BF16),
                 pltpu.VMEM((nchip * r2, 256), BF16),
                 pltpu.VMEM((nchip, 16, r2 // 16 * dh), BF16),
                 pltpu.VMEM((nchip, 16, r2 // 16 * dh), BF16),
@@ -366,10 +404,10 @@
                 pltpu.VMEM((2, r, d), F32),
                 pltpu.VMEM((r, d), F32),
                 pltpu.VMEM((r, d), BF16),
-                pltpu.VMEM((2, r2, cw), F32),
+                pltpu.VMEM((2, 2, r, cw), F32),
                 dma((6,)), dma((SLOTS,)), dma((nb,)), dma, dma,
-                dma((nchip,)), dma((nchip,)), dma((nchip,)), dma((nchip,)),
-                dma((d // cw,)), dma((d // cw,)), dma((2,)), dma,
+                dma((2, nchip)), dma((2, nchip)), dma((nchip,)), dma((nchip,)),
+                dma((d // cw,)), dma((d // cw,)), dma((3,)), dma((d // cw,)),
             ],
             compiler_params=pltpu.CompilerParams(
                 collective_id=0, has_side_effects=True, vmem_limit_bytes=67043328),

time: 52.9 us -> 47 us (0.89)
  Pallas kernels: 51.1 us -> 45.2 us
    pallas_call x1, Pallas kernels: 51.1 us -> 45.2 us  [local(): pl.pallas_call(functools.partial(_kernel, (r, d, nh, dh, f, nchip)), out_...]
where the time goes in v3:
time: 47 us; the launch traced here: 46.9 us
  Pallas kernels  45.2 us (96%)
  local copies, waits for them, and re-layouts  1.72 us (4%)
    pallas_call x1, Pallas kernels, local(): pl.pallas_call(functools.partial(_kernel, (r, d, nh, dh, f, nchip)), out_...  45.2 us
    unnamed x1, local copies, waits for them, and re-layouts  1.72 us

profile of v3, /device:TPU:97, one launch (start us, length us, event | category | flops | bytes accessed | tf_op | source)
XLA Modules:
  0.0 46.9 jit_solution(15195250088456928281)
XLA Ops:
  0.0 45.2 %layer.1 = bf16[64,2560]{1,0:T(8,128)(2,1)} custom-call(bf16[64,2560]{1,0:T(8,128)(2,1)} %x_hbm.1, f32[2560]{0:T(1024)} %g1_hbm.1, f32[2560]{0:T(1024)} %b1_hbm.1, f32[2560]{0:T(1024)} %g2_hbm.1, f32[2560]{0:T(1024)} %b2_hbm.1, f32[8,128]{1,0:T(8,128)} %constant.2.clone.inv_hbm, bf16[2560,7680]{1,0:T(8,128)(2,1)} %wqkv.1, bf16[2560,2560]{1,0:T(8,128)(2,1)} %bitcast.1, ...), custom_call_target="tpu_custom_call" | custom-call | flops 10066329600 | bytes 78643200 | tf_op jit(solution)/shard_map/layer/pallas_call | solution.py:381
  45.2 1.7 %copy.12 = bf16[64,2560]{1,0:T(8,128)(2,1)} copy(bf16[64,2560]{1,0:T(8,128)(2,1)} %layer.1) | data formatting | bytes 655360

commit v4 on v3

--- a/solution.py
+++ b/solution.py
@@ -17,6 +17,7 @@
 SLOTS = 6
 GH = 8
 KB = 512
+FAR = (4, 5, 3, 6, 2, 7, 1)
 
 
 def _gelu(x):
@@ -153,21 +154,21 @@
                     [pw[0][:, sl], pw[1][:, sl], pw[2][:, sl], jnp.zeros((r, 256 - 3 * dh), BF16)], axis=1)
 
     def q_sends(gg, halves):
-        def send(j, carry):
-            chip = owner(gg, lax.rem(j + me // ngrp, GH))
-
-            @pl.when(chip != me)
-            def _():
-                for which in halves:
-                    q_send(me, chip, which).start()
-
-            @pl.when(chip == me)
-            def _():
-                for which in halves:
-                    q_local(which).start()
-            return carry
-
-        lax.fori_loop(0, GH, send, 0)
+        for k in FAR:
+            chip = owner(gg, (k + me // ngrp) % GH)
+            for which in halves:
+                q_send(me, chip, which).start()
+        chip = owner(gg, me // ngrp)
+
+        @pl.when(chip != me)
+        def _():
+            for which in halves:
+                q_send(me, chip, which).start()
+
+        @pl.when(chip == me)
+        def _():
+            for which in halves:
+                q_local(which).start()
 
     parts = []
     qkv_copy(0, 0).wait()
@@ -214,11 +215,14 @@
         up(m)
         if refill:
             w1_copy(m + SLOTS).start(priority=1)
+        else:
+            @pl.when(m == nm - SLOTS)
+            def _():
+                for n in range(2, nb2 + nbo):
+                    b_copy(n).start(priority=1)
         return carry
 
     lax.fori_loop(1, nm - SLOTS, functools.partial(mlp1, True), 0)
-    for n in range(2, nb2 + nbo):
-        b_copy(n).start(priority=1)
     lax.fori_loop(nm - SLOTS, nm, functools.partial(mlp1, False), 0)
     act(nm - 1)
 
@@ -264,22 +268,22 @@
     og = r2 // 16
 
     def attend(i, carry):
-        us = [lax.rem(me + i + n, qper) for n in range(nq)]
-        blocks = [qper * n + us[n] for n in range(nq)]
+        u = (me + jnp.where(i == qper - 1, 0, jnp.where(i == qper - 2, qper - 1, qper - 2 - i))) % qper
+        blocks = [qper * n + u for n in range(nq)]
         row0 = [pl.multiple_of(j * r2, r2) for j in blocks]
         lq = []
         for n in range(nq):
             q = rbuf[pl.ds(row0[n], r2), 0:128]
             lq.append(jnp.concatenate(
                 [jnp.zeros((r2, dh), BF16), q[:, :dh], jnp.zeros((r2, 256 - 2 * dh), BF16)], axis=1))
-        ahead = lax.broadcasted_iota(jnp.int32, (r2, KB), 1) - lax.broadcasted_iota(jnp.int32, (r2, KB), 0)
+        seen = (lax.broadcasted_iota(jnp.int32, (r2, KB), 1) - lax.broadcasted_iota(jnp.int32, (r2, KB), 0)) <= u * r2
         sc = [[] for _ in range(nq)]
         for k in range(nq):
             t = lax.dot_general(jnp.concatenate(lq[k:], axis=0), rbuf[k * KB:(k + 1) * KB, :],
                                 (((1,), (1,)), ((), ())), preferred_element_type=F32)
             for n in range(k, nq):
                 tn = t[(n - k) * r2:(n - k + 1) * r2]
-                sc[n].append(jnp.where(ahead <= us[n] * r2, tn, NEG) if n == k else tn)
+                sc[n].append(jnp.where(seen, tn, NEG) if n == k else tn)
         for n in range(nq):
             mx = functools.reduce(jnp.maximum, sc[n])
             mx = jnp.max(mx, axis=-1, keepdims=True)
@@ -291,9 +295,7 @@
             obuf[blocks[n]] = jnp.concatenate(
                 [o[16 * g:16 * (g + 1), v0:v0 + dh] for g in range(og)], axis=1).astype(BF16)
 
-        def send(n, carry):
-            j = qper * n + lax.rem(me + i + n, qper)
-
+        for j in blocks:
             @pl.when(j != me)
             def _():
                 o_send(me, j).start()
@@ -301,9 +303,6 @@
             @pl.when(j == me)
             def _():
                 o_local().start()
-            return carry
-
-        lax.fori_loop(0, nq, send, 0)
         return carry
 
     lax.fori_loop(0, qper, attend, 0)

time: 47 us -> 42.2 us (0.90)
  Pallas kernels: 45.2 us -> 40.4 us
    pallas_call x1, Pallas kernels: 45.2 us -> 40.4 us  [local(): pl.pallas_call(functools.partial(_kernel, (r, d, nh, dh, f, nchip)), out_...]
where the time goes in v4:
time: 42.2 us; the launch traced here: 42.1 us
  Pallas kernels  40.4 us (96%)
  local copies, waits for them, and re-layouts  1.72 us (4%)
    pallas_call x1, Pallas kernels, local(): pl.pallas_call(functools.partial(_kernel, (r, d, nh, dh, f, nchip)), out_...  40.4 us
    unnamed x1, local copies, waits for them, and re-layouts  1.72 us

profile of v4, /device:TPU:97, one launch (start us, length us, event | category | flops | bytes accessed | tf_op | source)
XLA Modules:
  0.0 42.1 jit_solution(7524766111104245519)
XLA Ops:
  0.0 40.4 %layer.1 = bf16[64,2560]{1,0:T(8,128)(2,1)} custom-call(bf16[64,2560]{1,0:T(8,128)(2,1)} %x_hbm.1, f32[2560]{0:T(1024)} %g1_hbm.1, f32[2560]{0:T(1024)} %b1_hbm.1, f32[2560]{0:T(1024)} %g2_hbm.1, f32[2560]{0:T(1024)} %b2_hbm.1, f32[8,128]{1,0:T(8,128)} %constant.2.clone.inv_hbm, bf16[2560,7680]{1,0:T(8,128)(2,1)} %wqkv.1, bf16[2560,2560]{1,0:T(8,128)(2,1)} %bitcast.1, ...), custom_call_target="tpu_custom_call" | custom-call | flops 10066329600 | bytes 78643200 | tf_op jit(solution)/shard_map/layer/pallas_call | solution.py:380
  40.4 1.7 %copy.12 = bf16[64,2560]{1,0:T(8,128)(2,1)} copy(bf16[64,2560]{1,0:T(8,128)(2,1)} %layer.1) | data formatting | bytes 655360

commit v5 on v4

--- a/solution.py
+++ b/solution.py
@@ -14,9 +14,11 @@
 F32 = jnp.float32
 BF16 = jnp.bfloat16
 MESH = pl.DeviceIdType.MESH
-SLOTS = 6
+SLOTS = 5
 GH = 8
 KB = 512
+PW = 512
+OSLOT = 0
 FAR = (4, 5, 3, 6, 2, 7, 1)
 
 
@@ -24,9 +26,9 @@
     return 0.5 * x * (1.0 + lax.erf(x * np.float32(math.sqrt(0.5))))
 
 
-def _kernel(dims, x_hbm, g1_hbm, b1_hbm, g2_hbm, b2_hbm, inv_hbm, wqkv, wo, w1, w2, y_hbm,
-            xall, g1_v, b1_v, g2_v, b2_v, inv_v, a_v, m_v, t_v, h_v, aw, bw, sbuf, rbuf, obuf, orecv, ocat, yacc, yrecv, ybuf, cs,
-            small_sem, a_sem, b_sem, xs_sem, xr_sem, qs_sem, qr_sem, os_sem, or_sem, ys_sem, yr_sem, loc_sem, out_sem):
+def _kernel(dims, x_hbm, g1_hbm, b1_hbm, g2_hbm, b2_hbm, inv_hbm, wqkv, wo, w1, w2, y_ref,
+            xall, g1_v, b1_v, g2_v, b2_v, inv_v, a_v, m_v, h_v, aw, bw, sbuf, rbuf, obuf, orecv, yacc, yrecv, cs,
+            small_sem, a_sem, b_sem, xs_sem, xr_sem, qs_sem, qr_sem, os_sem, or_sem, ys_sem, yr_sem, loc_sem):
     r, d, nh, dh, f, nchip = dims
     half = dh // 2
     dc = d // 2
@@ -49,26 +51,32 @@
     def group(g):
         return (me % ngrp + me // (2 * ngrp) + g + 1) % ngrp
 
+    def q_block(n):
+        return aw.at[n] if n < SLOTS else bw.at[fc - d:fc, 0:cw]
+
     def qkv_copy(g, t):
         col = pl.multiple_of(t * d + c * dc + group(g) * cw, 128)
         n = 3 * g + t
-        return pltpu.make_async_copy(wqkv.at[:, pl.ds(col, cw)], aw.at[n], a_sem.at[n])
+        return pltpu.make_async_copy(wqkv.at[:, pl.ds(col, cw)], q_block(n), a_sem.at[n])
 
     def w1_copy(m):
         col = pl.multiple_of(c * fc + m * cw, 128)
-        n = lax.rem(m, SLOTS)
+        n = m % SLOTS
         return pltpu.make_async_copy(w1.at[:, pl.ds(col, cw)], aw.at[n], a_sem.at[n])
 
     nb2 = nm
-    nbo = dc // cw
+    nbo = d // PW
 
     def b_copy(n):
-        if n < nb2:
-            return pltpu.make_async_copy(w2.at[pl.ds(pl.multiple_of(c * fc + n * cw, 128), cw), :],
-                                         bw.at[pl.ds(n * cw, cw), :], b_sem.at[n])
-        k = n - nb2
-        return pltpu.make_async_copy(wo.at[pl.ds(pl.multiple_of(c * dc + k * cw, 128), cw), :],
+        return pltpu.make_async_copy(w2.at[pl.ds(pl.multiple_of(c * fc + n * cw, 128), cw), :],
                                      bw.at[pl.ds(n * cw, cw), :], b_sem.at[n])
+
+    def o_block(n):
+        return aw.at[OSLOT + n // 2, pl.ds(n % 2 * dc, dc), 0:PW]
+
+    def wo_copy(n):
+        return pltpu.make_async_copy(wo.at[pl.ds(pl.multiple_of(c * dc, 128), dc), pl.ds(n * PW, PW)],
+                                     o_block(n), b_sem.at[nb2 + n])
 
     smalls = [
         pltpu.make_async_copy(x_hbm, xall.at[c], small_sem.at[0]),
@@ -80,9 +88,8 @@
     ]
     for cp in smalls:
         cp.start()
-    for g in range(ngrp):
-        for t in range(3):
-            qkv_copy(g, t).start(priority=1)
+    for n in range(3 * ngrp):
+        qkv_copy(n // 3, n % 3).start(priority=1)
     for n in range(2):
         b_copy(n).start(priority=1)
 
@@ -133,7 +140,7 @@
             sbuf.at[me, which], rbuf.at[pl.ds(pl.multiple_of(me * r2 + which * r, r), r), :], loc_sem.at[which])
 
     def q_part(g, which, t):
-        part = jnp.dot(a_v[which], aw[3 * g + t], preferred_element_type=F32).astype(BF16)
+        part = jnp.dot(a_v[which], q_block(3 * g + t)[...], preferred_element_type=F32).astype(BF16)
         return rope(part, which) if t < 2 else part
 
     def q_pack(which, gg, parts):
@@ -144,7 +151,9 @@
 
     def q_group(g, gg):
         a = a_v[...].reshape(r2, d)
-        parts = [jnp.dot(a, aw[3 * g + t], preferred_element_type=F32).astype(BF16) for t in range(3)]
+        for t in range(3):
+            qkv_copy(g, t).wait()
+        parts = [jnp.dot(a, q_block(3 * g + t)[...], preferred_element_type=F32).astype(BF16) for t in range(3)]
         for which in range(2):
             pw = [p[which * r:(which + 1) * r] for p in parts]
             pw = [rope(pw[0], which), rope(pw[1], which), pw[2]]
@@ -188,22 +197,24 @@
     xcopy.wait()
     norms(1 - c)
     q_pack(1 - c, group(0), [q_part(0, 1 - c, t) for t in range(3)])
-    for t in range(3):
-        w1_copy(t).start(priority=1)
+    for n in range(3):
+        w1_copy(n).start(priority=1)
     q_sends(group(0), [1 - c])
     for g in range(1, ngrp):
-        for t in range(3):
-            qkv_copy(g, t).wait()
         q_group(g, group(g))
-        for t in range(3):
-            w1_copy(3 * g + t).start(priority=1)
+        for n in range(3 * g, min(3 * g + 3, SLOTS)):
+            w1_copy(n).start(priority=1)
         q_sends(group(g), [0, 1])
 
+    def pre(m):
+        return pl.ds(pl.multiple_of(m % 2 * cw, 128), cw)
+
     def up(m):
-        t_v[lax.rem(m, 2)] = jnp.dot(m_v[...].reshape(r2, d), aw[lax.rem(m, SLOTS)], preferred_element_type=F32)
+        t = jnp.dot(m_v[...].reshape(r2, d), aw[m % SLOTS], preferred_element_type=F32)
+        yacc[:, :, pre(m)] = t.reshape(2, r, cw)
 
     def act(m):
-        h_v[:, pl.ds(pl.multiple_of(m * cw, 128), cw)] = _gelu(t_v[lax.rem(m, 2)]).astype(BF16)
+        h_v[:, pl.ds(pl.multiple_of(m * cw, 128), cw)] = _gelu(yacc[:, :, pre(m)].reshape(r2, cw)).astype(BF16)
 
     w1_copy(0).wait()
     up(0)
@@ -218,12 +229,14 @@
         else:
             @pl.when(m == nm - SLOTS)
             def _():
-                for n in range(2, nb2 + nbo):
+                for n in range(2, nb2):
                     b_copy(n).start(priority=1)
         return carry
 
     lax.fori_loop(1, nm - SLOTS, functools.partial(mlp1, True), 0)
     lax.fori_loop(nm - SLOTS, nm, functools.partial(mlp1, False), 0)
+    for n in range(nbo):
+        wo_copy(n).start(priority=1)
     act(nm - 1)
 
     nt = d // 2
@@ -320,43 +333,31 @@
 
     lax.fori_loop(1, nchip, o_wait, 0)
     for g in range(og):
-        ocat[16 * g:16 * (g + 1), :] = jnp.concatenate(
+        a_v[16 * g // r, 16 * g % r:16 * g % r + 16, 0:dc] = jnp.concatenate(
             [orecv[owner(j // GH, j % GH)][:, g * dh:(g + 1) * dh] for j in range(nchip)], axis=1)
-    for n in range(nb2, nb2 + nbo):
-        b_copy(n).wait()
-
-    ny = 2
-    yw = d // ny
+    for n in range(nbo):
+        wo_copy(n).wait()
+
+    pieces = [(k, min(k + 2, nbo)) for k in range(0, nbo, 2)]
 
     def y_send(n):
-        cols = pl.ds(pl.multiple_of(n * yw, 128), yw)
+        cols = slice(pieces[n][0] * PW, pieces[n][1] * PW)
         return pltpu.make_async_remote_copy(
             src_ref=yacc.at[1 - c, :, cols], dst_ref=yrecv.at[:, cols],
             send_sem=ys_sem.at[n], recv_sem=yr_sem.at[n], device_id={"seq": partner}, device_id_type=MESH)
 
-    def proj(n, carry):
-        cols = pl.ds(pl.multiple_of(n * yw, 128), yw)
-        t = jnp.dot(ocat[...], bw[fc:fc + dc, cols], preferred_element_type=F32)
-        yacc[:, :, cols] = yacc[:, :, cols] + t.reshape(2, r, yw)
+    o_all = a_v[:, :, 0:dc].reshape(r2, dc)
+    for n, (k0, k1) in enumerate(pieces):
+        for k in range(k0, k1):
+            cols = slice(k * PW, (k + 1) * PW)
+            t = jnp.dot(o_all, o_block(k)[...], preferred_element_type=F32)
+            yacc[:, :, cols] = yacc[:, :, cols] + t.reshape(2, r, PW)
         y_send(n).start()
-        return carry
-
-    lax.fori_loop(0, ny, proj, 0)
-
-    def y_out(n):
-        cols = pl.ds(pl.multiple_of(n * yw, 128), yw)
-        return pltpu.make_async_copy(ybuf.at[:, cols], y_hbm.at[:, cols], out_sem.at[n])
-
-    def finish(n, carry):
-        cols = pl.ds(pl.multiple_of(n * yw, 128), yw)
+
+    for n, (k0, k1) in enumerate(pieces):
+        cols = slice(k0 * PW, k1 * PW)
         y_send(n).wait()
-        ybuf[:, cols] = (xall[c, :, cols].astype(F32) + yacc[c, :, cols] + yrecv[:, cols]).astype(BF16)
-        y_out(n).start()
-        return carry
-
-    lax.fori_loop(0, ny, finish, 0)
-    for n in range(ny):
-        y_out(n).wait()
+        y_ref[:, cols] = (xall[c, :, cols].astype(F32) + yacc[c, :, cols] + yrecv[:, cols]).astype(BF16)
 
 
 def solution(mesh):
@@ -374,14 +375,14 @@
         inv = np.concatenate([inv, inv, np.zeros(128 - dh)]).astype(np.float32)
         inv = jnp.asarray(np.tile(inv[None], (8, 1)))
         r2, cw, dc, fc = 2 * r, GH * dh, d // 2, f // 2
-        nb = (fc + dc) // cw
+        nb = fc // cw + d // PW
         dma = pltpu.SemaphoreType.DMA
         flops = 2 * r2 * (d * 3 * dc + d * fc * 2 + dc * d)
         return pl.pallas_call(
             functools.partial(_kernel, (r, d, nh, dh, f, nchip)),
             out_shape=jax.ShapeDtypeStruct((r, d), BF16),
             in_specs=[pl.BlockSpec(memory_space=pl.ANY)] * 10,
-            out_specs=pl.BlockSpec(memory_space=pl.ANY),
+            out_specs=pl.BlockSpec(memory_space=pltpu.VMEM),
             scratch_shapes=[
                 pltpu.VMEM((2, r, d), BF16),
                 pltpu.VMEM((d,), F32),
@@ -391,29 +392,26 @@
                 pltpu.VMEM((8, 128), F32),
                 pltpu.VMEM((2, r, d), BF16),
                 pltpu.VMEM((2, r, d), BF16),
-                pltpu.VMEM((2, r2, cw), F32),
                 pltpu.VMEM((r2, fc), BF16),
                 pltpu.VMEM((SLOTS, d, cw), BF16),
-                pltpu.VMEM((fc + dc, d), BF16),
+                pltpu.VMEM((fc, d), BF16),
                 pltpu.VMEM((nchip, 2, r, 256), BF16),
                 pltpu.VMEM((nchip * r2, 256), BF16),
                 pltpu.VMEM((nchip, 16, r2 // 16 * dh), BF16),
                 pltpu.VMEM((nchip, 16, r2 // 16 * dh), BF16),
-                pltpu.VMEM((r2, dc), BF16),
                 pltpu.VMEM((2, r, d), F32),
                 pltpu.VMEM((r, d), F32),
-                pltpu.VMEM((r, d), BF16),
                 pltpu.VMEM((2, 2, r, cw), F32),
-                dma((6,)), dma((SLOTS,)), dma((nb,)), dma, dma,
+                dma((6,)), dma((6,)), dma((nb,)), dma, dma,
                 dma((2, nchip)), dma((2, nchip)), dma((nchip,)), dma((nchip,)),
-                dma((d // cw,)), dma((d // cw,)), dma((3,)), dma((d // cw,)),
+                dma((d // cw,)), dma((d // cw,)), dma((3,)),
             ],
             compiler_params=pltpu.CompilerParams(
-                collective_id=0, has_side_effects=True, vmem_limit_bytes=67043328),
+                collective_id=0, has_side_effects=True, vmem_limit_bytes=55600000),
             cost_estimate=pl.CostEstimate(flops=flops, bytes_accessed=2 * (d * 3 * dc + d * f + dc * d), transcendentals=0),
             name="layer",
-        )(x, g1, b1, g2, b2, inv,
-          wqkv, wo.reshape(nh * dh, d), w1, w2)
+        )(*[pltpu.with_memory_space_constraint(v, pltpu.HBM)
+            for v in (x, g1, b1, g2, b2, inv, wqkv, wo.reshape(nh * dh, d), w1, w2)])
 
     rows = P(("data", "seq"), None)
     rep = P()

time: 42.2 us -> 40.2 us (0.953)
  Pallas kernels: 40.4 us -> 39.4 us
  local copies, waits for them, and re-layouts: 1.72 us -> 0.73 us
    unnamed x1, local copies, waits for them, and re-layouts: 1.72 us -> 0.73 us
    pallas_call x1, Pallas kernels: 40.4 us -> 39.4 us  [local(): pl.pallas_call(functools.partial(_kernel, (r, d, nh, dh, f, nchip)), out_...]
where the time goes in v5:
time: 40.2 us; the launch traced here: 40.1 us
  Pallas kernels  39.4 us (98%)
  local copies, waits for them, and re-layouts  0.73 us (2%)
    pallas_call x1, Pallas kernels, local(): pl.pallas_call(functools.partial(_kernel, (r, d, nh, dh, f, nchip)), out_...  39.4 us

profile of v5, /device:TPU:97, one launch (start us, length us, event | category | flops | bytes accessed | tf_op | source)
XLA Modules:
  0.0 40.1 jit_solution(10004196392063076431)
XLA Ops:
  0.0 39.4 %layer.1 = bf16[64,2560]{1,0:T(8,128)(2,1)S(1)} custom-call(bf16[64,2560]{1,0:T(8,128)(2,1)} %x_hbm.1, f32[2560]{0:T(1024)} %g1_hbm.1, f32[2560]{0:T(1024)} %b1_hbm.1, f32[2560]{0:T(1024)} %g2_hbm.1, f32[2560]{0:T(1024)} %b2_hbm.1, f32[8,128]{1,0:T(8,128)} %constant.2.clone.inv_hbm, bf16[2560,7680]{1,0:T(8,128)(2,1)} %wqkv.1, bf16[2560,2560]{1,0:T(8,128)(2,1)} %bitcast.1, ...), custom_call_target="tpu_custom_call" | custom-call | flops 10066329600 | bytes 78643200 | tf_op jit(solution)/shard_map/layer/pallas_call | solution.py:381
  39.4 0.7 %copy.12 = bf16[64,2560]{1,0:T(8,128)(2,1)} copy(bf16[64,2560]{1,0:T(8,128)(2,1)S(1)} %layer.1) | data formatting | bytes 655360

commit v6 on v5

--- a/solution.py
+++ b/solution.py
@@ -19,6 +19,7 @@
 KB = 512
 PW = 512
 OSLOT = 0
+DX = (2, 1, 3, 0)
 FAR = (4, 5, 3, 6, 2, 7, 1)
 
 
@@ -240,7 +241,7 @@
     act(nm - 1)
 
     nt = d // 2
-    early = 2
+    early = 3
 
     def down(k0, k1, first):
         def body(n, carry):
@@ -280,8 +281,8 @@
     nq = nchip // qper
     og = r2 // 16
 
-    def attend(i, carry):
-        u = (me + jnp.where(i == qper - 1, 0, jnp.where(i == qper - 2, qper - 1, qper - 2 - i))) % qper
+    def attend(dx):
+        u = (me + dx) % qper
         blocks = [qper * n + u for n in range(nq)]
         row0 = [pl.multiple_of(j * r2, r2) for j in blocks]
         lq = []
@@ -308,7 +309,14 @@
             obuf[blocks[n]] = jnp.concatenate(
                 [o[16 * g:16 * (g + 1), v0:v0 + dh] for g in range(og)], axis=1).astype(BF16)
 
+        return blocks
+
+    def o_sends(dx, blocks):
         for j in blocks:
+            if dx:
+                o_send(me, j).start()
+                continue
+
             @pl.when(j != me)
             def _():
                 o_send(me, j).start()
@@ -316,9 +324,12 @@
             @pl.when(j == me)
             def _():
                 o_local().start()
-        return carry
-
-    lax.fori_loop(0, qper, attend, 0)
+
+    first = [attend(dx) for dx in DX[:2]]
+    for dx, blocks in zip(DX[:2], first):
+        o_sends(dx, blocks)
+    for dx in DX[2:]:
+        o_sends(dx, attend(dx))
 
     for n in range(early, nb2):
         b_copy(n).wait()
@@ -368,7 +379,7 @@
         r, d = x.shape
         nh, dh, _ = wo.shape
         f = w1.shape[1]
-        if nh != nseq or nchip % GH or (KB % (2 * r)):
+        if nh != nseq or KB // (2 * r) != len(DX) or nchip % GH or (KB % (2 * r)):
             raise ValueError("unsupported sizes")
         half = dh // 2
         inv = 10000.0 ** (-2.0 * np.arange(half) / dh)

time: 40.2 us -> 39.8 us (0.990)
  no operation moved by 1% of the time
where the time goes in v6:
time: 39.8 us
  Pallas kernels  39 us (98%)
  local copies, waits for them, and re-layouts  0.73 us (2%)
    pallas_call x1, Pallas kernels, local(): pl.pallas_call(functools.partial(_kernel, (r, d, nh, dh, f, nchip)), out_...  39 us

profile of v6, /device:TPU:97, one launch (start us, length us, event | category | flops | bytes accessed | tf_op | source)
XLA Modules:
  0.0 39.8 jit_solution(3642435853992346829)
XLA Ops:
  0.0 39.0 %layer.1 = bf16[64,2560]{1,0:T(8,128)(2,1)S(1)} custom-call(bf16[64,2560]{1,0:T(8,128)(2,1)} %x_hbm.1, f32[2560]{0:T(1024)} %g1_hbm.1, f32[2560]{0:T(1024)} %b1_hbm.1, f32[2560]{0:T(1024)} %g2_hbm.1, f32[2560]{0:T(1024)} %b2_hbm.1, f32[8,128]{1,0:T(8,128)} %constant.2.clone.inv_hbm, bf16[2560,7680]{1,0:T(8,128)(2,1)} %wqkv.1, bf16[2560,2560]{1,0:T(8,128)(2,1)} %bitcast.1, ...), custom_call_target="tpu_custom_call" | custom-call | flops 10066329600 | bytes 78643200 | tf_op jit(solution)/shard_map/layer/pallas_call | solution.py:392
  39.0 0.7 %copy.12 = bf16[64,2560]{1,0:T(8,128)(2,1)} copy(bf16[64,2560]{1,0:T(8,128)(2,1)S(1)} %layer.1) | data formatting | bytes 655360

commit v7 on v6

--- a/solution.py
+++ b/solution.py
@@ -19,7 +19,7 @@
 KB = 512
 PW = 512
 OSLOT = 0
-DX = (2, 1, 3, 0)
+DX = (1, 3, 2, 0)
 FAR = (4, 5, 3, 6, 2, 7, 1)
 
 

time: 39.8 us -> 39.4 us (0.990)
  Pallas kernels: 39 us -> 38.6 us
    pallas_call x1, Pallas kernels: 39 us -> 38.6 us  [local(): pl.pallas_call(functools.partial(_kernel, (r, d, nh, dh, f, nchip)), out_...]
where the time goes in v7:
time: 39.4 us; the launch traced here: 39.3 us
  Pallas kernels  38.6 us (98%)
  local copies, waits for them, and re-layouts  0.73 us (2%)
    pallas_call x1, Pallas kernels, local(): pl.pallas_call(functools.partial(_kernel, (r, d, nh, dh, f, nchip)), out_...  38.6 us

profile of v7, /device:TPU:97, one launch (start us, length us, event | category | flops | bytes accessed | tf_op | source)
XLA Modules:
  0.0 39.3 jit_solution(11291639604721540184)
XLA Ops:
  0.0 38.6 %layer.1 = bf16[64,2560]{1,0:T(8,128)(2,1)S(1)} custom-call(bf16[64,2560]{1,0:T(8,128)(2,1)} %x_hbm.1, f32[2560]{0:T(1024)} %g1_hbm.1, f32[2560]{0:T(1024)} %b1_hbm.1, f32[2560]{0:T(1024)} %g2_hbm.1, f32[2560]{0:T(1024)} %b2_hbm.1, f32[8,128]{1,0:T(8,128)} %constant.2.clone.inv_hbm, bf16[2560,7680]{1,0:T(8,128)(2,1)} %wqkv.1, bf16[2560,2560]{1,0:T(8,128)(2,1)} %bitcast.1, ...), custom_call_target="tpu_custom_call" | custom-call | flops 10066329600 | bytes 78643200 | tf_op jit(solution)/shard_map/layer/pallas_call | solution.py:392
  38.6 0.7 %copy.12 = bf16[64,2560]{1,0:T(8,128)(2,1)} copy(bf16[64,2560]{1,0:T(8,128)(2,1)S(1)} %layer.1) | data formatting | bytes 655360
